TPU v7x, 32 devices: a whole 2x2x4 slice. The times are simulated.
32 devices in a mesh: angle: 8 (over y, x, core), scan: 4 (over z).
Axes of the slice: x: 2, y: 2, z: 4, core: 2. Of those that a mesh axis runs over, the one named last changes fastest.
Arguments:
- object_slices: float32 [2, 3, 256, 512], P(None, None, 'scan', 'angle'), may hold values from -5 to 5
- probe: float32 [2, 128, 128], replicated, may hold values from -6 to 6
- intensities: float32 [8, 4, 2, 128, 128], P('angle', 'scan'), may hold values from 0.5 to 3.5
- row_offsets: int32 [8, 4, 2], P('angle', 'scan'), may hold values from 0 to 64
- column_starts: int32 [8, 4, 2], P('angle', 'scan'), may hold values from 0 to 320
- slice_shifts: int32 [8, 3], P('angle'), may hold values from 0 to 64
- counts: int32 [8, 4], P('angle', 'scan'), may hold values from 1 to 2, as said below
Outputs:
- object_gradient: float32 [2, 3, 256, 512], P(None, None, 'scan', 'angle')
- probe_gradient: float32 [2, 128, 128], replicated
Inputs may be any that keep to these rules, and one draw needn't show every extreme that they name: `counts`: the largest value 2 occurs in every draw.
All inputs are finite; a program needn't handle non-finite values.
Results may differ from a plain program's by a relative error of at most 0.0003.
Values sent between devices are 32-bit elements; how exact they have to be, the bound alone decides.
A program may use at most 64 MiB of HBM per device.

v0:
```python
from functools import partial

import jax
import jax.numpy as jnp
from jax import lax
from jax.sharding import PartitionSpec as P


def padded(cells, sides, width):
    for axis, dim in sides:
        count = lax.axis_size(axis)
        ends = count - 1
        head = lax.slice_in_dim(cells, 0, width, axis=dim)
        tail = lax.slice_in_dim(cells, cells.shape[dim] - width, cells.shape[dim], axis=dim)
        cells = jnp.concatenate(
            [
                lax.ppermute(tail, axis, [(i, (i + 1) % count) for i in range(ends)]),
                cells,
                lax.ppermute(head, axis, [((i + 1) % count, i) for i in range(ends)]),
            ],
            axis=dim,
        )
    return cells


def propagator(size):
    index = jnp.arange(size, dtype=jnp.int32)
    centred = ((index + size // 2) % size - size // 2).astype(jnp.float32)
    radius = centred[:, None] * centred[:, None] + centred[None, :] * centred[None, :]
    phase = 8.0 * jnp.pi * radius / (size * size)
    return (jnp.cos(phase), jnp.sin(phase))


def tables(size):
    index = jnp.arange(size, dtype=jnp.int32)
    turns = index[:, None] * index[None, :] % size
    phase = 2.0 * jnp.pi * turns.astype(jnp.float32) / size
    scale = 1.0 / jnp.sqrt(jnp.float32(size))
    return (jnp.cos(phase) * scale, jnp.sin(phase) * scale)


def matmul(first, second):
    return jnp.dot(
        first, second, precision=lax.Precision.HIGHEST, preferred_element_type=jnp.float32
    )


def transform(real_part, imag_part, cosine, sine, sign):
    left_re = matmul(cosine, real_part) - sign * matmul(sine, imag_part)
    left_im = matmul(cosine, imag_part) + sign * matmul(sine, real_part)
    right_re = matmul(left_re, cosine) - sign * matmul(left_im, sine)
    right_im = matmul(left_im, cosine) + sign * matmul(left_re, sine)
    return (right_re, right_im)


def local_loss(slab, probe, measured, weight, cosine, sine, kern_re, kern_im):
    wave_re, wave_im = (probe[0], probe[1])
    layers = slab.shape[1]
    for k in range(layers):
        object_re, object_im = (slab[0, k], slab[1, k])
        wave_re, wave_im = (
            wave_re * object_re - wave_im * object_im,
            wave_re * object_im + wave_im * object_re,
        )
        if k + 1 < layers:
            freq_re, freq_im = transform(wave_re, wave_im, cosine, sine, -1.0)
            freq_re, freq_im = (
                freq_re * kern_re - freq_im * kern_im,
                freq_re * kern_im + freq_im * kern_re,
            )
            wave_re, wave_im = transform(freq_re, freq_im, cosine, sine, 1.0)
    far_re, far_im = transform(wave_re, wave_im, cosine, sine, -1.0)
    differ = far_re * far_re + far_im * far_im - measured
    return weight * jnp.sum(differ * differ)


def local(object_slices, probe, intensities, row_offsets, column_starts, slice_shifts, counts):
    band = object_slices.shape[2]
    framed = padded(object_slices, (("scan", 2),), band)
    region = lax.all_gather(framed, "angle", axis=3, tiled=True)
    size = probe.shape[1]
    slots = row_offsets.shape[2]
    layers = region.shape[1]
    angles = lax.axis_size("angle")
    cosine, sine = tables(size)
    kern_re, kern_im = propagator(size)
    shifts = slice_shifts[0]
    zero = jnp.zeros((), jnp.int32)

    def visit(slot, carry):
        gradient_region, gradient_probe = carry
        top = row_offsets[0, 0, slot]
        start = column_starts[0, 0, slot]
        slab = jnp.concatenate(
            [
                lax.dynamic_slice(
                    region, (zero, zero + k, top, start + shifts[k]), (2, 1, size, size)
                )
                for k in range(layers)
            ],
            axis=1,
        )
        weight = jnp.where(slot < counts[0, 0], 0.5 / angles, 0.0).astype(jnp.float32)
        measured = intensities[0, 0, slot]
        scorer = partial(
            local_loss,
            measured=measured,
            weight=weight,
            cosine=cosine,
            sine=sine,
            kern_re=kern_re,
            kern_im=kern_im,
        )
        loss, pull = jax.vjp(scorer, slab, probe)
        slab_grad, probe_grad = pull(jnp.ones_like(loss))
        for k in range(layers):
            place = (zero, zero + k, top, start + shifts[k])
            current = lax.dynamic_slice(gradient_region, place, (2, 1, size, size))
            gradient_region = lax.dynamic_update_slice(
                gradient_region, current + slab_grad[:, k : k + 1], place
            )
        return (gradient_region, gradient_probe + probe_grad)

    start_carry = (jnp.zeros(region.shape, jnp.float32), jnp.zeros(probe.shape, jnp.float32))
    gradient_region, gradient_probe = lax.fori_loop(0, slots, visit, start_carry)
    shared = lax.psum_scatter(gradient_region, "angle", scatter_dimension=3, tiled=True)
    edges = jnp.concatenate([shared[:, :, :band], shared[:, :, 2 * band :]], axis=2)
    rimmed = padded(edges, (("scan", 2),), band)
    object_gradient = shared[:, :, band : 2 * band] + rimmed[:, :, :band] + rimmed[:, :, 3 * band :]
    group_total = lax.psum(gradient_probe, "scan")
    probe_gradient = lax.psum(group_total, "angle")
    return (object_gradient, probe_gradient)


def solution(mesh):
    return jax.shard_map(
        local,
        mesh=mesh,
        in_specs=(
            P(None, None, "scan", "angle"),
            P(),
            P("angle", "scan", None, None, None),
            P("angle", "scan", None),
            P("angle", "scan", None),
            P("angle", None),
            P("angle", "scan"),
        ),
        out_specs=(P(None, None, "scan", "angle"), P()),
        check_vma=False,
    )
```

profile of v0, /device:TPU:0, one launch (start us, length us, event | category | flops | bytes accessed | tf_op | source)
XLA Modules:
  0.0 352.7 jit_solution(17662193562692884179)
XLA Ops:
  7.2 1.1 copy.25
  8.3 1.3 collective-permute-start.1
  9.6 5.6 %collective-permute-start = (f32[2,3,64,64]{2,0,1,3:T(2,128)S(1)}, f32[2,3,64,64]{2,0,1,3:T(2,128)S(1)}, u32[]{:S(2)}, u32[]{:S(2)}) collective-permute-start(f32[2,3,64,64]{2,0,1,3:T(2,128)S(1)} %copy.25), channel_id=1, source_target_pairs={{0,1},{1,2},{2,3},{4,5},{5,6},{6,7},{8,9},{9,10},{10,11},{12,13},{... | collective-permute-start | bytes 294920 | tf_op jit(solution)/shard_map/ppermute | solution.py:17
  15.2 2.9 collective-permute-done.1
  18.2 1.2 collective-permute-done
  19.3 1.2 pad_maximum_fusion
  20.7 34.6 %all-gather.2.cloned.1.call-done = f32[2,3,192,512]{2,0,1,3:T(2,128)} async-done(((f32[2,3,192,64]{2,0,1,3:T(2,128)}), f32[2,3,192,512]{2,0,1,3:T(2,128)}) %all-gather.2.cloned.1.call-update) | async-done | bytes 2359312 | tf_op jit(solution)/shard_map/all_gather | solution.py:80
  55.2 5.6 %copy.28 = f32[2,3,192,512]{3,2,1,0:T(8,128)} copy(f32[2,3,192,512]{2,0,1,3:T(2,128)} %all-gather.2.cloned.1.call-done) | data formatting | bytes 4718592
  61.8 136.3 %while.19 = (s32[]{:T(128)}, f32[2,3,192,512]{3,2,1,0:T(8,128)S(1)}, f32[2,128,128]{2,1,0:T(8,128)S(1)}, s32[1,1,2]{2,1,0:T(1,128)S(1)}, s32[1,1,2]{2,1,0:T(1,12...) while((s32[]{:T(128)}, ...), condition=%wide.region_1.2_spmd.clone.clone.clone.clone, body=%wide.region_0.1_spmd.clone.clone.clone.clone.sunk | while | flops 2037301248 | bytes 20128300 | solution.py:125
  69.6 1.1 fusion.857
  74.6 0.8 fusion.868
  75.5 0.8 convolution_add_fusion.36
  76.8 0.8 fusion.866
  77.6 0.8 convolution_subtract_fusion.8
  79.3 1.5 multiply_add_fusion.7
  84.7 0.8 fusion.880
  85.5 1.3 convolution_add_fusion.37
  87.3 0.8 fusion.878
  88.2 0.8 convolution_subtract_fusion.10
  89.9 1.5 multiply_subtract_fusion.3
  99.0 1.5 add_bitcast_fusion.9
  104.8 0.8 fusion.902
  105.6 0.8 convolution_add_fusion.43
  107.2 0.8 convolution_add_fusion.42
  109.5 1.5 add_bitcast_fusion.10
  115.2 0.8 fusion.913
  116.0 0.8 convolution_add_fusion.47
  117.5 0.8 convolution_add_fusion.46
  120.1 1.5 add_bitcast_fusion.11
  121.8 2.2 dynamic_update_slice.36
  124.1 2.2 dynamic_update_slice.37
  126.4 2.2 dynamic_update_slice.38
  136.7 1.1 fusion.857
  141.7 0.8 fusion.868
  142.5 0.8 convolution_add_fusion.36
  143.8 0.8 fusion.866
  144.6 0.8 convolution_subtract_fusion.8
  146.4 1.5 multiply_add_fusion.7
  151.8 0.8 fusion.880
  152.6 1.0 convolution_add_fusion.37
  154.1 0.8 fusion.878
  154.9 0.8 convolution_subtract_fusion.10
  156.6 1.5 multiply_subtract_fusion.3
  165.7 1.5 add_bitcast_fusion.9
  171.6 0.8 fusion.902
  172.4 0.8 convolution_add_fusion.43
  173.9 0.8 convolution_add_fusion.42
  176.3 1.5 add_bitcast_fusion.10
  182.0 0.8 fusion.913
  184.3 0.8 convolution_add_fusion.46
  186.1 0.9 fusion.914
  187.0 1.5 add_bitcast_fusion.11
  188.8 2.2 dynamic_update_slice.36
  191.1 2.2 dynamic_update_slice.37
  193.3 2.2 dynamic_update_slice.38
  198.2 3.4 copy.37
  201.6 6.0 %reshape.42 = f32[512,1152]{1,0:T(8,128)} reshape(f32[512,2,3,192]{3,2,1,0:T(4,128)} %bitcast.367) | data formatting | bytes 4718592
  208.4 42.3 %reduce-scatter.4.cloned.1.call-done = f32[64,1152]{1,0:T(8,128)} async-done(((f32[512,1152]{1,0:T(8,128)}), f32[64,1152]{1,0:T(8,128)}) %reduce-scatter.4.cloned.1.call-update) | async-done | bytes 294928
  250.7 1.3 reshape.43
  252.6 1.3 collective-permute-start.3
  253.9 4.6 %collective-permute-start.2 = (f32[2,3,64,64]{3,2,1,0:T(8,128)S(1)}, f32[2,3,64,64]{3,2,1,0:T(8,128)S(1)}, u32[]{:S(2)}, u32[]{:S(2)}) collective-permute-start(f32[2,3,64,64]{3,2,1,0:T(8,128)S(1)} %copy.40), channel_id=1, source_target_pairs={{0,1},{1,2},{2,3},{4,5},{5,6},{6,7},{8,9},{9,10},{10,11},{12,13},{... | collective-permute-start | bytes 294920 | tf_op jit(solution)/shard_map/ppermute | solution.py:17
  258.4 29.9 %all-reduce.11.cloned.1.call-done = f32[2,128,128]{2,1,0:T(8,128)} async-done(((f32[2,128,128]{2,1,0:T(8,128)}), f32[2,128,128]{2,1,0:T(8,128)}) %all-reduce.11.cloned.1.call-update) | async-done | bytes 131088 | tf_op jit(solution)/shard_map/psum | solution.py:130
  289.2 55.2 %all-reduce.13.cloned.1.call-done = f32[2,128,128]{2,1,0:T(8,128)} async-done(((f32[2,128,128]{2,1,0:T(8,128)}), f32[2,128,128]{2,1,0:T(8,128)}) %all-reduce.13.cloned.1.call-update) | async-done | bytes 131088 | tf_op jit(solution)/shard_map/psum | solution.py:131
  344.4 1.6 copy.56
  (166 shorter events, 69.4 us)
Async XLA Ops:
  7.2 48.1 %all-gather.2.cloned.1.call-start = ((), (), s32[]{:S(2)}) async-start(), calls=%async_computation.1 | async-start | bytes 3538944 | tf_op jit(solution)/shard_map/all_gather | solution.py:80
  8.3 9.9 %collective-permute-start.1 = (f32[2,3,64,64]{2,0,1,3:T(2,128)S(1)}, f32[2,3,64,64]{2,0,1,3:T(2,128)S(1)}, u32[]{:S(2)}, u32[]{:S(2)}) collective-permute-start(f32[2,3,64,64]{2,0,1,3:T(2,128)S(1)} %copy.25), channel_id=1, source_target_pairs={{1,0},{2,1},{3,2},{5,4},{6,5},{7,6},{9,8},{10,9},{11,10},{13,12},{... | collective-permute-start | bytes 294920 | tf_op jit(solution)/shard_map/ppermute | solution.py:19
  9.6 9.7 %collective-permute-start = (f32[2,3,64,64]{2,0,1,3:T(2,128)S(1)}, f32[2,3,64,64]{2,0,1,3:T(2,128)S(1)}, u32[]{:S(2)}, u32[]{:S(2)}) collective-permute-start(f32[2,3,64,64]{2,0,1,3:T(2,128)S(1)} %copy.25), channel_id=1, source_target_pairs={{0,1},{1,2},{2,3},{4,5},{5,6},{6,7},{8,9},{9,10},{10,11},{12,13},{... | collective-permute-start | bytes 294920 | tf_op jit(solution)/shard_map/ppermute | solution.py:17
  20.6 230.1 %reduce-scatter.4.cloned.1.call-start = ((), (), s32[]{:S(2)}) async-start(), calls=%async_computation.4 | async-start | bytes 2654208
  60.8 0.9 copy-start
  60.8 0.9 copy-start.2
  60.8 0.9 copy-start.3
  60.8 0.9 copy-start.4
  60.8 1.0 copy-start.5
  198.2 3.4 copy-start.1
  207.6 80.7 %all-reduce.11.cloned.1.call-start = ((), (), s32[]{:S(2)}) async-start(), calls=%async_computation.2 | async-start | bytes 262144 | tf_op jit(solution)/shard_map/psum | solution.py:130
  208.4 136.0 %all-reduce.13.cloned.1.call-start = ((), (), s32[]{:S(2)}) async-start(), calls=%async_computation.3 | async-start | bytes 262144 | tf_op jit(solution)/shard_map/psum | solution.py:131
  252.6 35.9 %collective-permute-start.3 = (f32[2,3,64,64]{3,2,1,0:T(8,128)S(1)}, f32[2,3,64,64]{3,2,1,0:T(8,128)S(1)}, u32[]{:S(2)}, u32[]{:S(2)}) collective-permute-start(f32[2,3,64,64]{3,2,1,0:T(8,128)S(1)} %copy.41), channel_id=1, source_target_pairs={{1,0},{2,1},{3,2},{5,4},{6,5},{7,6},{9,8},{10,9},{11,10},{13,12},{... | collective-permute-start | bytes 294920 | tf_op jit(solution)/shard_map/ppermute | solution.py:19
  253.9 34.6 %collective-permute-start.2 = (f32[2,3,64,64]{3,2,1,0:T(8,128)S(1)}, f32[2,3,64,64]{3,2,1,0:T(8,128)S(1)}, u32[]{:S(2)}, u32[]{:S(2)}) collective-permute-start(f32[2,3,64,64]{3,2,1,0:T(8,128)S(1)} %copy.40), channel_id=1, source_target_pairs={{0,1},{1,2},{2,3},{4,5},{5,6},{6,7},{8,9},{9,10},{10,11},{12,13},{... | collective-permute-start | bytes 294920 | tf_op jit(solution)/shard_map/ppermute | solution.py:17
Sparse Core Ops, SparseCore 0:
  20.7 34.4 all-gather.1
  207.7 42.9 reduce-scatter.3
  253.6 34.6 all-reduce.10
  291.2 53.1 all-reduce.12
where the time goes:
time: 355 us; the launch traced here: 353 us
  waiting for transfers between devices  167 us (47%)
  matrix products  101 us (28%)
  local copies, waits for them, and re-layouts  36.1 us (10%)
  loops' own time  16.9 us (5%)
  between operations  14.1 us (4%)
  starting transfers between devices  12.9 us (4%)
  other arithmetic  4.95 us (1%)
    dot_general x160, matrix products, matmul(): jnp.dot(first, second, precision=lax.Precision.HIGHEST, preferred_element...  101 us
    psum x1, waiting for transfers between devices, local(): probe_gradient = lax.psum(group_total, 'angle')  55.2 us
    unnamed x5, waiting for transfers between devices  43.1 us
    all_gather x1, waiting for transfers between devices, local(): region = lax.all_gather(framed, 'angle', axis=3, tiled=True)  34.6 us
    psum x1, waiting for transfers between devices, local(): group_total = lax.psum(gradient_probe, 'scan')  29.9 us
    unnamed x21, local copies, waits for them, and re-layouts  20.1 us
    another operation x1, loops' own time, local(): lax.fori_loop(0, slots, visit, start_carry)  16.9 us
    dynamic_update_slice x6, local copies, waits for them, and re-layouts, visit(): lax.dynamic_update_slice(gradient_region, current + slab_grad[:, k:k + 1]...  13 us
  transfers between devices with their start and end apart: 8, of which 6 were waited for; matrix products, arithmetic and copies ran while one was open for 1% of the time, Pallas kernels for 0%

commit v1 on v0

--- a/solution.py
+++ b/solution.py
@@ -2,8 +2,172 @@
 
 import jax
 import jax.numpy as jnp
+import ml_dtypes
+import numpy as np
 from jax import lax
+from jax.experimental import pallas as pl
+from jax.experimental.pallas import tpu as pltpu
 from jax.sharding import PartitionSpec as P
+
+
+def shifted(cells, axis, step):
+    count = lax.axis_size(axis)
+    ends = count - 1
+    if step > 0:
+        pairs = [(i, (i + 1) % count) for i in range(ends)]
+    else:
+        pairs = [((i + 1) % count, i) for i in range(ends)]
+    return lax.ppermute(cells, axis, pairs)
+
+
+def operators(size):
+    index = np.arange(size)
+    turns = np.outer(index, index) % size
+    fourier = np.exp(-2j * np.pi * turns / size) / np.sqrt(size)
+    centred = (index + size // 2) % size - size // 2
+    factor = np.exp(8j * np.pi * centred**2 / size**2)
+    step = np.conj(fourier) @ (factor[:, None] * fourier)
+    packed = []
+    for matrix in (step, fourier):
+        right = np.block([[matrix.real, matrix.imag], [-matrix.imag, matrix.real]])
+        packed.append(right)
+        packed.append(right.T)
+    out = np.zeros((4, 2, 2 * size, 2 * size), ml_dtypes.bfloat16)
+    for i, matrix in enumerate(packed):
+        whole = matrix.astype(np.float32)
+        high = whole.astype(ml_dtypes.bfloat16)
+        out[i, 0] = high
+        out[i, 1] = (whole - high.astype(np.float32)).astype(ml_dtypes.bfloat16)
+    return out
+
+
+def halves(x):
+    high = x.astype(jnp.bfloat16)
+    return high, (x - high.astype(jnp.float32)).astype(jnp.bfloat16)
+
+
+def dot(a, b):
+    return jnp.dot(a, b, preferred_element_type=jnp.float32)
+
+
+def both_sides(waves, right, left):
+    size = waves[0][0].shape[0]
+    stacked = jnp.concatenate([jnp.concatenate([re, im], axis=1) for re, im in waves], axis=0)
+    high, low = halves(stacked)
+    out = dot(high, right[0]) + (dot(low, right[0]) + dot(high, right[1]))
+    rows = [out[s * size : (s + 1) * size] for s in range(len(waves))]
+    beside = jnp.concatenate(
+        [
+            jnp.concatenate([r[:, :size] for r in rows], axis=1),
+            jnp.concatenate([r[:, size:] for r in rows], axis=1),
+        ],
+        axis=0,
+    )
+    high, low = halves(beside)
+    out = dot(left[0], high) + (dot(left[0], low) + dot(left[1], high))
+    return [
+        (out[:size, s * size : (s + 1) * size], out[size:, s * size : (s + 1) * size])
+        for s in range(len(waves))
+    ]
+
+
+def times(a, b):
+    return (a[0] * b[0] - a[1] * b[1], a[0] * b[1] + a[1] * b[0])
+
+
+def conj_times(a, b):
+    return (a[0] * b[0] + a[1] * b[1], a[0] * b[1] - a[1] * b[0])
+
+
+def compute_kernel(
+    angles, rows_ref, cols_ref, shifts_ref, counts_ref, region_ref, probe_ref, measured_ref, mats_ref,
+    grad_ref, probe_grad_ref,
+):
+    blocks, layers, height, lanes = region_ref.shape
+    width = lanes // 2
+    size = probe_ref.shape[1]
+    slots = measured_ref.shape[0]
+    lane = lax.broadcasted_iota(jnp.int32, (size, lanes), 1)
+    lower = lane < width
+    swap = lambda x: pltpu.roll(x, width, 1)
+    tops = [rows_ref[s] for s in range(slots)]
+    starts = [[cols_ref[s] + shifts_ref[k] for k in range(layers)] for s in range(slots)]
+
+    def place(s, k):
+        q = starts[s][k] // width
+        return q, starts[s][k] - q * width
+
+    def patch(s, k):
+        q, r = place(s, k)
+        rows = pl.ds(tops[s], size)
+        first = region_ref[q, k, rows, :]
+        second = region_ref[q + 1, k, rows, :]
+        third = region_ref[jnp.minimum(q + 2, blocks - 1), k, rows, :]
+        back = lax.rem(lanes - r, lanes)
+        inside = lane < lanes - r
+        pieces = []
+        for near, far in (
+            (jnp.where(lower, first, swap(second)), third),
+            (jnp.where(lower, swap(first), second), swap(third)),
+        ):
+            pieces.append(jnp.where(inside, pltpu.roll(near, back, 1), pltpu.roll(far, back, 1)))
+        return tuple(pieces)
+
+    objects = [[patch(s, k) for k in range(layers)] for s in range(slots)]
+    step_r, step_l, four_r, four_l = [(mats_ref[i, 0], mats_ref[i, 1]) for i in range(4)]
+    waves = [(probe_ref[0], probe_ref[1])] * slots
+    before = []
+    for k in range(layers):
+        before.append(waves)
+        waves = [times(waves[s], objects[s][k]) for s in range(slots)]
+        if k + 1 < layers:
+            waves = both_sides(waves, step_r, step_l)
+    far = both_sides(waves, four_r, four_l)
+    grads = []
+    for s in range(slots):
+        weight = jnp.where(s < counts_ref[0], 2.0 / angles, 0.0)
+        re, im = far[s]
+        scale = weight * (re * re + im * im - measured_ref[s])
+        grads.append((scale * re, scale * im))
+    grads = both_sides(grads, four_l, four_r)
+    grad_ref[...] = jnp.zeros(grad_ref.shape, jnp.float32)
+    for k in reversed(range(layers)):
+        for s in range(slots):
+            re, im = conj_times(before[k][s], grads[s])
+            q, r = place(s, k)
+            rows = pl.ds(tops[s], size)
+            re, im = pltpu.roll(re, r, 1), pltpu.roll(im, r, 1)
+            zero = jnp.zeros_like(re)
+            near_re, near_im = jnp.where(lane >= r, re, zero), jnp.where(lane >= r, im, zero)
+            far_re, far_im = jnp.where(lane < r, re, zero), jnp.where(lane < r, im, zero)
+            grad_ref[q, k, rows, :] += jnp.where(lower, near_re, swap(near_im))
+            grad_ref[q + 1, k, rows, :] += jnp.where(lower, swap(near_re), near_im)
+            last = jnp.minimum(q + 2, blocks - 1)
+            grad_ref[last, k, rows, :] += jnp.where(lower, far_re, swap(far_im))
+        grads = [conj_times(objects[s][k], grads[s]) for s in range(slots)]
+        if k > 0:
+            grads = both_sides(grads, step_l, step_r)
+    probe_grad_ref[0] = sum(g[0] for g in grads)
+    probe_grad_ref[1] = sum(g[1] for g in grads)
+
+
+def gradients(region, probe, intensities, row_offsets, column_starts, slice_shifts, counts):
+    angles = lax.axis_size("angle")
+    smem = pl.BlockSpec(memory_space=pltpu.SMEM)
+    vmem = pl.BlockSpec(memory_space=pltpu.VMEM)
+    return pl.pallas_call(
+        partial(compute_kernel, angles),
+        out_shape=(
+            jax.ShapeDtypeStruct(region.shape, jnp.float32),
+            jax.ShapeDtypeStruct(probe.shape, jnp.float32),
+        ),
+        in_specs=[smem] * 4 + [vmem] * 4,
+        out_specs=(vmem, vmem),
+        compiler_params=pltpu.CompilerParams(vmem_limit_bytes=48 * 2**20),
+    )(
+        row_offsets.reshape(-1), column_starts.reshape(-1), slice_shifts.reshape(-1),
+        counts.reshape(-1), region, probe, intensities[0, 0], jnp.asarray(operators(probe.shape[1])),
+    )
 
 
 def padded(cells, sides, width):
@@ -74,7 +238,7 @@
     return weight * jnp.sum(differ * differ)
 
 
-def local(object_slices, probe, intensities, row_offsets, column_starts, slice_shifts, counts):
+def general(object_slices, probe, intensities, row_offsets, column_starts, slice_shifts, counts):
     band = object_slices.shape[2]
     framed = padded(object_slices, (("scan", 2),), band)
     region = lax.all_gather(framed, "angle", axis=3, tiled=True)
@@ -132,6 +296,36 @@
     return (object_gradient, probe_gradient)
 
 
+def packable(object_slices, probe):
+    size = probe.shape[1]
+    band, width = object_slices.shape[2:]
+    return 2 * width == size == 128 and band % 8 == 0 and lax.axis_size("angle") >= 4
+
+
+def local(object_slices, probe, intensities, row_offsets, column_starts, slice_shifts, counts):
+    args = (object_slices, probe, intensities, row_offsets, column_starts, slice_shifts, counts)
+    if not packable(object_slices, probe):
+        return general(*args)
+    band = object_slices.shape[2]
+    width = object_slices.shape[3]
+    packed = jnp.concatenate([object_slices[0], object_slices[1]], axis=-1)
+    framed = jnp.concatenate(
+        [shifted(packed, "scan", 1), packed, shifted(packed, "scan", -1)], axis=1
+    )
+    region = lax.all_gather(framed, "angle", axis=0)
+    grad, probe_grad = gradients(
+        region, probe, intensities, row_offsets, column_starts, slice_shifts, counts
+    )
+    shared = lax.psum_scatter(grad, "angle", scatter_dimension=0, tiled=False)
+    total = (
+        shared[:, band : 2 * band]
+        + shifted(shared[:, 2 * band :], "scan", 1)
+        + shifted(shared[:, :band], "scan", -1)
+    )
+    object_gradient = jnp.stack([total[:, :, :width], total[:, :, width:]])
+    return (object_gradient, lax.psum(lax.psum(probe_grad, "scan"), "angle"))
+
+
 def solution(mesh):
     return jax.shard_map(
         local,

time: 355 us -> 206 us (0.58)
  matrix products: 101 us -> 0 us
  local copies, waits for them, and re-layouts: 36.1 us -> 9.08 us
  loops' own time: 16.9 us -> 0 us
  Pallas kernels: 0 us -> 6.48 us
  waiting for transfers between devices: 167 us -> 162 us
    dot_general x160 -> x0, matrix products: 101 us -> none  [matmul(): jnp.dot(first, second, precision=lax.Precision.HIGHEST, preferred_element...]
    unnamed x5 -> x4, waiting for transfers between devices: 43.1 us -> 0.73 us
    reduce_scatter x0 -> x1, waiting for transfers between devices: none -> 41.7 us  [local(): shared = lax.psum_scatter(grad, 'angle', scatter_dimension=0, tiled=False)]
    another operation x1 -> x0, loops' own time: 16.9 us -> none  [local(): lax.fori_loop(0, slots, visit, start_carry)]
    unnamed x21 -> x15, local copies, waits for them, and re-layouts: 20.1 us -> 7.01 us
    dynamic_update_slice x6 -> x0, local copies, waits for them, and re-layouts: 13 us -> none  [visit(): lax.dynamic_update_slice(gradient_region, current + slab_grad[:, k:k + 1]...]
    pallas_call x0 -> x1, Pallas kernels: none -> 6.48 us  [gradients(): pl.pallas_call(partial(compute_kernel, angles), out_shape=(jax.ShapeDtype...]
    all_gather x1, waiting for transfers between devices: 34.6 us -> 30.9 us  [local(): region = lax.all_gather(framed, 'angle', axis=0)]
where the time goes in v1:
time: 206 us
  waiting for transfers between devices  162 us (79%)
  between operations  14.5 us (7%)
  starting transfers between devices  11.7 us (6%)
  local copies, waits for them, and re-layouts  9.08 us (4%)
  Pallas kernels  6.48 us (3%)
  other arithmetic  2.51 us (1%)
    psum x2, waiting for transfers between devices, local(): return (object_gradient, lax.psum(lax.psum(probe_grad, 'scan'), 'angle'))  86.2 us
    reduce_scatter x1, waiting for transfers between devices, local(): shared = lax.psum_scatter(grad, 'angle', scatter_dimension=0, tiled=False)  41.7 us
    all_gather x1, waiting for transfers between devices, local(): region = lax.all_gather(framed, 'angle', axis=0)  30.9 us
    ppermute x4, starting transfers between devices, shifted(): return lax.ppermute(cells, axis, pairs)  11.6 us
    unnamed x15, local copies, waits for them, and re-layouts  7.01 us
    pallas_call x1, Pallas kernels, gradients(): pl.pallas_call(partial(compute_kernel, angles), out_shape=(jax.ShapeDtype...  6.48 us
  transfers between devices with their start and end apart: 8, of which 6 were waited for; matrix products, arithmetic and copies ran while one was open for 1% of the time, Pallas kernels for 0%

profile of v1, /device:TPU:0, one launch (start us, length us, event | category | flops | bytes accessed | tf_op | source)
XLA Modules:
  0.0 206.0 jit_solution(15943906205949214516)
XLA Ops:
  7.2 0.0 copy-start.1
  7.2 0.0 all-gather.3.cloned.1.call-start
  7.2 1.0 slice_bitcast_fusion.3
  8.3 0.1 pad_maximum_fusion.2
  8.4 1.3 collective-permute-start.1
  9.7 5.6 %collective-permute-start = (f32[3,64,128]{2,1,0:T(8,128)S(1)}, f32[3,64,128]{2,1,0:T(8,128)S(1)}, u32[]{:S(2)}, u32[]{:S(2)}) collective-permute-start(f32[3,64,128]{2,1,0:T(8,128)S(1)} %pad_maximum_fusion.2), channel_id=1, source_target_pairs={{0,1},{1,2},{2,3},{4,5},{5,6},{6,7},{8,9},{9,10},{10,11},{12,13},{... | collective-permute-start | bytes 294920 | tf_op jit(solution)/shard_map/ppermute | solution.py:20
  15.3 0.8 collective-permute-done.1
  16.1 1.3 collective-permute-done
  17.4 0.8 pad_maximum_fusion
  18.3 0.0 all-gather.3.cloned.1.call-update
  18.3 0.0 reduce-scatter.2.cloned.1.call-start
  19.0 30.9 %all-gather.3.cloned.1.call-done = f32[24,192,128]{2,1,0:T(8,128)} async-done(((f32[3,192,128]{2,1,0:T(8,128)}), f32[24,192,128]{2,1,0:T(8,128)}) %all-gather.3.cloned.1.call-update) | async-done | bytes 2359312 | tf_op jit(solution)/shard_map/all_gather | solution.py:315
  49.8 0.0 copy-done.1
  49.8 0.0 copy-start
  49.8 1.7 copy-done
  51.5 0.0 copy-start.2
  51.5 0.9 copy-done.2
  52.4 0.0 copy-start.3
  52.4 0.9 copy-done.3
  53.3 0.0 copy-start.4
  53.3 0.7 copy-done.4
  54.0 0.0 copy-start.5
  54.0 0.7 copy-done.5
  54.6 0.0 copy-start.6
  54.6 0.7 copy-done.6
  55.3 6.5 %shard_map.95 = (f32[8,3,192,128]{3,2,1,0:T(8,128)}, f32[2,128,128]{2,1,0:T(8,128)}) custom-call(s32[2]{0:T(128)S(1)} %bitcast.18, s32[2]{0:T(128)S(1)} %bitcast.19, s32[3]{0:T(128)S(1)} %bitcast.20, s32[1]{0:T(128)} %bitcast.15.counts_ref, f32[8,3,192,128]{3,2,1,0:T(8,128)S(1)} %bitcast.16, f32[2,128,128]{2,1,0:T(8,128)S(1)} %copy-done.2, ...), custom_call_target="tpu_custom_call" | custom-call | tf_op jit(solution)/shard_map/pallas_call | solution.py:158
  61.8 0.0 reduce-scatter.2.cloned.1.call-update
  61.8 0.0 all-reduce.3.cloned.1.call-start
  61.8 0.7 all-reduce.3.cloned.1.call-update
  62.5 0.0 all-reduce.5.cloned.1.call-start
  62.6 41.7 %reduce-scatter.2.cloned.1.call-done = f32[1,3,192,128]{3,2,1,0:T(8,128)} async-done(((f32[8,3,192,128]{3,2,1,0:T(8,128)}), f32[1,3,192,128]{3,2,1,0:T(8,128)}) %reduce-scatter.2.cloned.1.call-update) | async-done | bytes 294928 | tf_op jit(solution)/shard_map/reduce_scatter | solution.py:319
  104.3 1.0 fusion.1
  105.2 3.4 %collective-permute-start.2 = (f32[3,64,128]{2,1,0:T(8,128)S(1)}, f32[3,64,128]{2,1,0:T(8,128)S(1)}, u32[]{:S(2)}, u32[]{:S(2)}) collective-permute-start(f32[3,64,128]{2,1,0:T(8,128)S(1)} %get-tuple-element.6), channel_id=1, source_target_pairs={{0,1},{1,2},{2,3},{4,5},{5,6},{6,7},{8,9},{9,10},{10,11},{12,13},{... | collective-permute-start | bytes 294920 | tf_op jit(solution)/shard_map/ppermute | solution.py:20
  108.6 1.3 collective-permute-start.3
  109.9 31.9 %all-reduce.3.cloned.1.call-done = f32[2,128,128]{2,1,0:T(8,128)} async-done(((f32[2,128,128]{2,1,0:T(8,128)}), f32[2,128,128]{2,1,0:T(8,128)}) %all-reduce.3.cloned.1.call-update) | async-done | bytes 131088 | tf_op jit(solution)/shard_map/psum | solution.py:326
  141.8 0.0 all-reduce.5.cloned.1.call-update
  141.9 0.0 collective-permute-done.2
  141.9 0.0 collective-permute-done.3
  141.9 0.9 fusion
  142.8 0.1 slice_bitcast_fusion.1
  142.9 0.7 pad_maximum_fusion.1
  143.6 54.3 %all-reduce.5.cloned.1.call-done = f32[2,128,128]{2,1,0:T(8,128)} async-done(((f32[2,128,128]{2,1,0:T(8,128)}), f32[2,128,128]{2,1,0:T(8,128)}) %all-reduce.5.cloned.1.call-update) | async-done | bytes 131088 | tf_op jit(solution)/shard_map/psum | solution.py:326
  197.9 1.6 copy.13
Async XLA Ops:
  7.2 42.7 %copy-start.1 = (bf16[4,2,256,256]{3,2,1,0:T(8,128)(2,1)S(1)}, bf16[4,2,256,256]{3,2,1,0:T(8,128)(2,1)}, u32[]{:S(2)}) copy-start(bf16[4,2,256,256]{3,2,1,0:T(8,128)(2,1)} %constant.2.clone.mats_ref) | copy-start | bytes 3145732
  7.2 42.6 %all-gather.3.cloned.1.call-start = ((), (), s32[]{:S(2)}) async-start(), calls=%async_computation.4 | async-start | bytes 2654208 | tf_op jit(solution)/shard_map/all_gather | solution.py:315
  8.4 7.7 %collective-permute-start.1 = (f32[3,64,128]{2,1,0:T(8,128)S(1)}, f32[3,64,128]{2,1,0:T(8,128)S(1)}, u32[]{:S(2)}, u32[]{:S(2)}) collective-permute-start(f32[3,64,128]{2,1,0:T(8,128)S(1)} %pad_maximum_fusion.2), channel_id=1, source_target_pairs={{1,0},{2,1},{3,2},{5,4},{6,5},{7,6},{9,8},{10,9},{11,10},{13,12},{... | collective-permute-start | bytes 294920 | tf_op jit(solution)/shard_map/ppermute | solution.py:20
  9.7 7.8 %collective-permute-start = (f32[3,64,128]{2,1,0:T(8,128)S(1)}, f32[3,64,128]{2,1,0:T(8,128)S(1)}, u32[]{:S(2)}, u32[]{:S(2)}) collective-permute-start(f32[3,64,128]{2,1,0:T(8,128)S(1)} %pad_maximum_fusion.2), channel_id=1, source_target_pairs={{0,1},{1,2},{2,3},{4,5},{5,6},{6,7},{8,9},{9,10},{10,11},{12,13},{... | collective-permute-start | bytes 294920 | tf_op jit(solution)/shard_map/ppermute | solution.py:20
  18.3 86.0 %reduce-scatter.2.cloned.1.call-start = ((), (), s32[]{:S(2)}) async-start(), calls=%async_computation.1 | async-start | bytes 2654208 | tf_op jit(solution)/shard_map/reduce_scatter | solution.py:319
  49.8 1.7 copy-start
  51.5 0.9 copy-start.2
  52.4 0.9 copy-start.3
  53.3 0.7 copy-start.4
  54.0 0.7 copy-start.5
  54.6 0.7 copy-start.6
  61.8 80.1 %all-reduce.3.cloned.1.call-start = ((), (), s32[]{:S(2)}) async-start(), calls=%async_computation.2 | async-start | bytes 262144 | tf_op jit(solution)/shard_map/psum | solution.py:326
  62.5 135.4 %all-reduce.5.cloned.1.call-start = ((), (), s32[]{:S(2)}) async-start(), calls=%async_computation.3 | async-start | bytes 262144 | tf_op jit(solution)/shard_map/psum | solution.py:326
  105.2 36.6 %collective-permute-start.2 = (f32[3,64,128]{2,1,0:T(8,128)S(1)}, f32[3,64,128]{2,1,0:T(8,128)S(1)}, u32[]{:S(2)}, u32[]{:S(2)}) collective-permute-start(f32[3,64,128]{2,1,0:T(8,128)S(1)} %get-tuple-element.6), channel_id=1, source_target_pairs={{0,1},{1,2},{2,3},{4,5},{5,6},{6,7},{8,9},{9,10},{10,11},{12,13},{... | collective-permute-start | bytes 294920 | tf_op jit(solution)/shard_map/ppermute | solution.py:20
  108.6 33.3 %collective-permute-start.3 = (f32[3,64,128]{2,1,0:T(8,128)S(1)}, f32[3,64,128]{2,1,0:T(8,128)S(1)}, u32[]{:S(2)}, u32[]{:S(2)}) collective-permute-start(f32[3,64,128]{2,1,0:T(8,128)S(1)} %get-tuple-element.7), channel_id=1, source_target_pairs={{1,0},{2,1},{3,2},{5,4},{6,5},{7,6},{9,8},{10,9},{11,10},{13,12},{... | collective-permute-start | bytes 294920 | tf_op jit(solution)/shard_map/ppermute | solution.py:20
Sparse Core Ops, SparseCore 0:
  18.4 31.3 all-gather.2
  61.9 42.3 reduce-scatter.1
  107.2 34.6 all-reduce.2
  144.7 53.1 all-reduce.4

commit v2 on v1

--- a/solution.py
+++ b/solution.py
@@ -8,16 +8,6 @@
 from jax.experimental import pallas as pl
 from jax.experimental.pallas import tpu as pltpu
 from jax.sharding import PartitionSpec as P
-
-
-def shifted(cells, axis, step):
-    count = lax.axis_size(axis)
-    ends = count - 1
-    if step > 0:
-        pairs = [(i, (i + 1) % count) for i in range(ends)]
-    else:
-        pairs = [((i + 1) % count, i) for i in range(ends)]
-    return lax.ppermute(cells, axis, pairs)
 
 
 def operators(size):
@@ -170,6 +160,277 @@
     )
 
 
+MESH = pl.DeviceIdType.MESH
+
+
+def flip(j, bit):
+    return j + bit * (1 - 2 * lax.rem(lax.div(j, bit), 2))
+
+
+def places():
+    me, z = lax.axis_index("angle"), lax.axis_index("scan")
+    x, y = flip(me, 2), flip(me, 4)
+    return me, z, lax.rem(me, 2), (me, x, y, flip(x, 4))
+
+
+def exchange(src, dst, send_sem, recv_sem, device):
+    return pltpu.make_async_remote_copy(
+        src_ref=src, dst_ref=dst, send_sem=send_sem, recv_sem=recv_sem, device_id=device,
+        device_id_type=MESH,
+    )
+
+
+def gather_kernel(scans, object_ref, region_ref, stage, z_sem, plane_sem, core_sem, recv_sem):
+    band, width = object_ref.shape[2:]
+    me, z, core, spots = places()
+    partner = flip(me, 1)
+    above, below = z > 0, z < scans - 1
+    for k in range(object_ref.shape[1]):
+        packed = jnp.concatenate([object_ref[0, k], object_ref[1, k]], axis=1)
+        stage[k] = packed
+        region_ref[me, k, band : 2 * band] = packed
+    barrier = pltpu.get_barrier_semaphore()
+
+    def greet(device):
+        pl.semaphore_signal(barrier, inc=1, device_id=device, device_id_type=MESH)
+
+    for peer in (partner, spots[1], spots[2]):
+        greet((peer, z))
+    pl.when(above)(lambda: greet((me, z - 1)))
+    pl.when(below)(lambda: greet((me, z + 1)))
+    zeros = jnp.zeros(region_ref.shape[:2] + (band,) + region_ref.shape[3:], jnp.float32)
+
+    @pl.when(jnp.logical_not(above))
+    def _():
+        region_ref[:, :, :band] = zeros
+
+    @pl.when(jnp.logical_not(below))
+    def _():
+        region_ref[:, :, 2 * band :] = zeros
+
+    pl.semaphore_wait(barrier, 3 + above.astype(jnp.int32) + below.astype(jnp.int32))
+
+    def piece(j, part):
+        return region_ref.at[j, :, pl.ds(part * band, band), :]
+
+    def to(src, j, part, sem, device):
+        return exchange(src, piece(j, part), sem, recv_sem.at[part, j], device)
+
+    def arrive(j, part):
+        to(piece(j, part), j, part, core_sem.at[0, 0], (partner, z)).wait_recv()
+
+    pending = []
+
+    def upright(i, src):
+        up = to(src, spots[i], 2, z_sem.at[0, i], (me, z - 1))
+        down = to(src, spots[i], 0, z_sem.at[1, i], (me, z + 1))
+        pl.when(above)(lambda: up.start())
+        pl.when(below)(lambda: down.start())
+        pending.append((above, up))
+        pending.append((below, down))
+
+    def share(i, part, src):
+        copy = to(src, spots[i], part, core_sem.at[part, i], (partner, z))
+        copy.start()
+        pending.append((None, copy))
+
+    def across(src, j, n, device):
+        copy = to(src, j, 1, plane_sem.at[n], (device, z))
+        copy.start()
+        pending.append((None, copy))
+
+    across(stage, me, 0, spots[1])
+    across(stage, me, 1, spots[2])
+    upright(0, stage)
+    share(0, 1, stage)
+    arrive(spots[1], 1)
+    upright(1, piece(spots[1], 1))
+    arrive(spots[2], 1)
+    source = spots[1] + core * (spots[2] - spots[1])
+    target = spots[2] + core * (spots[1] - spots[2])
+    across(piece(source, 1), source, 2, target)
+    upright(2, piece(spots[2], 1))
+    share(1, 1, piece(spots[1], 1))
+    share(2, 1, piece(spots[2], 1))
+    arrive(spots[3], 1)
+    upright(3, piece(spots[3], 1))
+    share(3, 1, piece(spots[3], 1))
+    for i in range(4):
+        for part, when in ((0, above), (2, below)):
+
+            copy = to(piece(spots[i], part), spots[i], part, core_sem.at[part, i], (partner, z))
+            pending.append((when, copy))
+
+            @pl.when(when)
+            def _(i=i, part=part, copy=copy):
+                arrive(spots[i], part)
+                copy.start()
+
+    for part, when in ((1, None), (0, above), (2, below)):
+        for i in range(4):
+            wait = partial(arrive, spots[i] + 1 - 2 * core, part)
+            wait() if when is None else pl.when(when)(wait)
+    for when, copy in pending:
+        copy.wait_send() if when is None else pl.when(when)(lambda copy=copy: copy.wait_send())
+
+
+def reduce_kernel(
+    scans, grad_ref, probe_ref, object_ref, total_ref,
+    core_in, held, z_in, ready, plane_in, last_in, passed, probe_in, scan_in, mine,
+    core_sem, z_sem, plane_sem, angle_sem, scan_sem, all_sem,
+):
+    angles, layers, height, lanes = grad_ref.shape
+    band = height // 3
+    rows = probe_ref.shape[0] // angles
+    me, z, core, spots = places()
+    partner = flip(me, 1)
+    above, below = z > 0, z < scans - 1
+    barrier = pltpu.get_barrier_semaphore()
+    peers = [lax.rem(me + d, angles) for d in range(1, angles)]
+    levels = [lax.rem(z + d, scans) for d in range(1, scans)]
+    for device in [(peer, z) for peer in peers] + [(me, level) for level in levels]:
+        pl.semaphore_signal(barrier, inc=1, device_id=device, device_id_type=MESH)
+    pl.semaphore_wait(barrier, angles + scans - 2)
+    pending = []
+
+    def go(src, dst, send_sem, recv_sem, device):
+        copy = exchange(src, dst, send_sem, recv_sem, device)
+        copy.start()
+        pending.append((None, copy))
+
+    def arrive(dst, recv_sem):
+        exchange(dst, dst, core_sem.at[0, 0], recv_sem, (partner, z)).wait_recv()
+
+    order = (3, 1, 2, 0)
+    for i in order:
+        go(grad_ref.at[spots[i] + 1 - 2 * core], core_in.at[i], core_sem.at[0, i], core_sem.at[1, i], (partner, z))
+    for d, peer in enumerate(peers):
+        go(
+            probe_ref.at[pl.ds(peer * rows, rows)], probe_in.at[me],
+            angle_sem.at[0, d], angle_sem.at[1, me], (peer, z),
+        )
+    for i in order:
+        arrive(core_in.at[i], core_sem.at[1, i])
+        for part in (0, 2, 1):
+            span = pl.ds(part * band, band)
+            held[i, :, span] = grad_ref[spots[i], :, span] + core_in[i, :, span]
+        up = exchange(
+            held.at[i, :, pl.ds(0, band)], z_in.at[1, i], z_sem.at[0, 0, i], z_sem.at[1, 1, i], (me, z - 1)
+        )
+        down = exchange(
+            held.at[i, :, pl.ds(2 * band, band)], z_in.at[0, i], z_sem.at[0, 1, i], z_sem.at[1, 0, i], (me, z + 1)
+        )
+        pl.when(above)(lambda up=up: up.start())
+        pl.when(below)(lambda down=down: down.start())
+        pending.append((above, up))
+        pending.append((below, down))
+    for peer in peers:
+        arrive(probe_in.at[peer], angle_sem.at[1, peer])
+    probe_in[me] = probe_ref[pl.ds(me * rows, rows)]
+    part_sum = probe_in[0]
+    for j in range(1, angles):
+        part_sum += probe_in[j]
+    passed[...] = part_sum
+    scan_in[z] = part_sum
+    for d, level in enumerate(levels):
+        go(passed, scan_in.at[z], scan_sem.at[0, d], scan_sem.at[1, z], (me, level))
+    first, second = 2 - core, 1 + core
+    near = spots[2] + core * (spots[1] - spots[2])
+    other = spots[1] + core * (spots[2] - spots[1])
+    for i in order:
+        ready[i] = held[i, :, pl.ds(band, band)]
+
+        @pl.when(above)
+        def _():
+            arrive(z_in.at[0, i], z_sem.at[1, 0, i])
+            ready[i] += z_in[0, i]
+
+        @pl.when(below)
+        def _():
+            arrive(z_in.at[1, i], z_sem.at[1, 1, i])
+            ready[i] += z_in[1, i]
+
+        if i == 3:
+            go(ready.at[3], plane_in.at[1], plane_sem.at[0, 1], plane_sem.at[1, 1], (near, z))
+        if i == 2:
+            go(ready.at[first], plane_in.at[0], plane_sem.at[0, 0], plane_sem.at[1, 0], (near, z))
+    arrive(plane_in.at[1], plane_sem.at[1, 1])
+    mine[...] = ready[second] + plane_in[1]
+    go(mine, last_in, plane_sem.at[0, 2], plane_sem.at[1, 2], (other, z))
+    for level in levels:
+        arrive(scan_in.at[level], scan_sem.at[1, level])
+    whole = scan_in[0]
+    for j in range(1, scans):
+        whole += scan_in[j]
+    own = pl.ds(me * rows, rows)
+    total_ref[own] = whole
+    passed_all = total_ref.at[own]
+    for d, peer in enumerate(peers):
+        go(passed_all, total_ref.at[own], all_sem.at[0, d], all_sem.at[1, me], (peer, z))
+    arrive(plane_in.at[0], plane_sem.at[1, 0])
+    arrive(last_in, plane_sem.at[1, 2])
+    result = ready[0] + plane_in[0] + last_in[...]
+    object_ref[0] = result[:, :, : lanes // 2]
+    object_ref[1] = result[:, :, lanes // 2 :]
+    for peer in peers:
+        arrive(total_ref.at[pl.ds(peer * rows, rows)], all_sem.at[1, peer])
+    for when, copy in pending:
+        copy.wait_send() if when is None else pl.when(when)(lambda copy=copy: copy.wait_send())
+
+
+def gather(object_slices):
+    angles, scans = lax.axis_size("angle"), lax.axis_size("scan")
+    parts, layers, band, width = object_slices.shape
+    vmem = pl.BlockSpec(memory_space=pltpu.VMEM)
+    dma = pltpu.SemaphoreType.DMA
+    return pl.pallas_call(
+        partial(gather_kernel, scans),
+        out_shape=jax.ShapeDtypeStruct((angles, layers, 3 * band, 2 * width), jnp.float32),
+        in_specs=[vmem],
+        out_specs=vmem,
+        scratch_shapes=[
+            pltpu.VMEM((layers, band, 2 * width), jnp.float32),
+            dma((2, 4)), dma((3,)), dma((3, 4)), dma((3, angles)),
+        ],
+        compiler_params=pltpu.CompilerParams(
+            collective_id=0, has_side_effects=True, vmem_limit_bytes=32 * 2**20
+        ),
+    )(object_slices)
+
+
+def reduce(grad, probe_grad):
+    angles, scans = lax.axis_size("angle"), lax.axis_size("scan")
+    layers, height, lanes = grad.shape[1:]
+    band = height // 3
+    flat = probe_grad.reshape(-1, probe_grad.shape[-1])
+    rows = flat.shape[0] // angles
+    block = (layers, band, lanes)
+    small = (rows, flat.shape[1])
+    vmem = pl.BlockSpec(memory_space=pltpu.VMEM)
+    dma = pltpu.SemaphoreType.DMA
+    buffer = lambda *shape: pltpu.VMEM(shape, jnp.float32)
+    object_grad, total = pl.pallas_call(
+        partial(reduce_kernel, scans),
+        out_shape=(
+            jax.ShapeDtypeStruct((2, layers, band, lanes // 2), jnp.float32),
+            jax.ShapeDtypeStruct(flat.shape, jnp.float32),
+        ),
+        in_specs=[vmem, vmem],
+        out_specs=(vmem, vmem),
+        scratch_shapes=[
+            buffer(4, layers, height, lanes), buffer(4, layers, height, lanes), buffer(2, 4, *block),
+            buffer(4, *block), buffer(2, *block), buffer(*block), buffer(*small),
+            buffer(angles, *small), buffer(scans, *small), buffer(*block),
+            dma((2, 4)), dma((2, 2, 4)), dma((2, 3)), dma((2, angles)), dma((2, scans)),
+            dma((2, angles)),
+        ],
+        compiler_params=pltpu.CompilerParams(
+            collective_id=1, has_side_effects=True, vmem_limit_bytes=32 * 2**20
+        ),
+    )(grad, flat)
+    return object_grad, total.reshape(probe_grad.shape)
+
+
 def padded(cells, sides, width):
     for axis, dim in sides:
         count = lax.axis_size(axis)
@@ -299,31 +560,18 @@
 def packable(object_slices, probe):
     size = probe.shape[1]
     band, width = object_slices.shape[2:]
-    return 2 * width == size == 128 and band % 8 == 0 and lax.axis_size("angle") >= 4
+    return 2 * width == size == 128 and band % 8 == 0 and lax.axis_size("angle") == 2**3
 
 
 def local(object_slices, probe, intensities, row_offsets, column_starts, slice_shifts, counts):
     args = (object_slices, probe, intensities, row_offsets, column_starts, slice_shifts, counts)
     if not packable(object_slices, probe):
         return general(*args)
-    band = object_slices.shape[2]
-    width = object_slices.shape[3]
-    packed = jnp.concatenate([object_slices[0], object_slices[1]], axis=-1)
-    framed = jnp.concatenate(
-        [shifted(packed, "scan", 1), packed, shifted(packed, "scan", -1)], axis=1
-    )
-    region = lax.all_gather(framed, "angle", axis=0)
+    region = gather(object_slices)
     grad, probe_grad = gradients(
         region, probe, intensities, row_offsets, column_starts, slice_shifts, counts
     )
-    shared = lax.psum_scatter(grad, "angle", scatter_dimension=0, tiled=False)
-    total = (
-        shared[:, band : 2 * band]
-        + shifted(shared[:, 2 * band :], "scan", 1)
-        + shifted(shared[:, :band], "scan", -1)
-    )
-    object_gradient = jnp.stack([total[:, :, :width], total[:, :, width:]])
-    return (object_gradient, lax.psum(lax.psum(probe_grad, "scan"), "angle"))
+    return reduce(grad, probe_grad)
 
 
 def solution(mesh):

time: 206 us -> 45.7 us (0.22)
  waiting for transfers between devices: 162 us -> 0 us
  Pallas kernels: 6.48 us -> 41.8 us
  between operations: 14.5 us -> 1.47 us
  starting transfers between devices: 11.7 us -> 0 us
  local copies, waits for them, and re-layouts: 9.08 us -> 2.28 us
  other arithmetic: 2.51 us -> 0 us
    psum x2 -> x0, waiting for transfers between devices: 86.2 us -> none  [local(): return (object_gradient, lax.psum(lax.psum(probe_grad, 'scan'), 'angle'))]
    reduce_scatter x1 -> x0, waiting for transfers between devices: 41.7 us -> none  [local(): shared = lax.psum_scatter(grad, 'angle', scatter_dimension=0, tiled=False)]
    pallas_call x0 -> x2, Pallas kernels: none -> 36.7 us  [the longest x1 19.8 us: reduce(): pl.pallas_call(partial(reduce_kernel, scans), out_shape=(jax.ShapeDtypeSt...]
    all_gather x1 -> x0, waiting for transfers between devices: 30.9 us -> none  [local(): region = lax.all_gather(framed, 'angle', axis=0)]
    ppermute x4 -> x0, starting transfers between devices: 11.6 us -> none  [shifted(): return lax.ppermute(cells, axis, pairs)]
    unnamed x15 -> x16, local copies, waits for them, and re-layouts: 7.01 us -> 2.28 us
    ppermute x4 -> x0, waiting for transfers between devices: 2.2 us -> none  [shifted(): return lax.ppermute(cells, axis, pairs)]
  transfers between devices with their start and end apart: 8 -> 0, of which waited for: 6 -> 0; matrix products, arithmetic and copies ran while one was open for 1% -> 0% of each run, Pallas kernels for 0% -> 0%
where the time goes in v2:
time: 45.7 us; the launch traced here: 45.5 us
  Pallas kernels  41.8 us (91%)
  local copies, waits for them, and re-layouts  2.28 us (5%)
  between operations  1.47 us (3%)
    pallas_call x1, Pallas kernels, reduce(): pl.pallas_call(partial(reduce_kernel, scans), out_shape=(jax.ShapeDtypeSt...  19.8 us
    pallas_call x1, Pallas kernels, gather(): pl.pallas_call(partial(gather_kernel, scans), out_shape=jax.ShapeDtypeStr...  16.9 us
    pallas_call x1, Pallas kernels, gradients(): pl.pallas_call(partial(compute_kernel, angles), out_shape=(jax.ShapeDtype...  5.09 us
    unnamed x16, local copies, waits for them, and re-layouts  2.28 us

profile of v2, /device:TPU:0, one launch (start us, length us, event | category | flops | bytes accessed | tf_op | source)
XLA Modules:
  0.0 45.5 jit_solution(11889649588084793058)
XLA Ops:
  0.6 0.0 copy-start
  1.4 0.0 copy-start.1
  1.4 0.9 %copy-done.1 = f32[2,3,64,64]{3,2,1,0:T(8,128)S(1)} copy-done((f32[2,3,64,64]{3,2,1,0:T(8,128)S(1)}, f32[2,3,64,64]{3,2,1,0:T(8,128)}, u32[]{:S(2)}) %copy-start.1) | copy-done | bytes 98328
  2.3 0.0 copy-start.2
  2.3 0.0 copy-start.3
  2.3 0.0 copy-start.4
  2.3 0.0 copy-start.5
  2.3 0.0 copy-start.6
  2.3 16.9 %shard_map.95.region_ref = f32[8,3,192,128]{3,2,1,0:T(8,128)S(1)} custom-call(f32[2,3,64,64]{3,2,1,0:T(8,128)S(1)} %copy-done.1), custom_call_target="tpu_custom_call" | custom-call | tf_op jit(solution)/shard_map/pallas_call | solution.py:386
  19.2 0.0 copy-done
  19.3 0.0 copy-done.2
  19.3 0.0 copy-done.3
  19.3 0.0 copy-done.4
  19.3 0.0 copy-done.5
  19.3 0.0 copy-done.6
  19.3 5.1 %shard_map.96 = (f32[8,3,192,128]{3,2,1,0:T(8,128)S(1)}, f32[2,128,128]{2,1,0:T(8,128)S(1)}) custom-call(s32[2]{0:T(128)S(1)} %bitcast.11, s32[2]{0:T(128)S(1)} %bitcast.12, s32[3]{0:T(128)S(1)} %bitcast.13, s32[1]{0:T(128)} %bitcast.7.counts_ref, f32[8,3,192,128]{3,2,1,0:T(8,128)S(1)} %shard_map.95.region_ref, f32[2,128,128]{2,1,0:T(8,128)S(1)} %copy-done.2, ...), custom_call_target="tpu_custom_call" | custom-call | tf_op jit(solution)/shard_map/pallas_call | solution.py:148
  24.4 19.8 %shard_map.97 = (f32[2,3,64,64]{3,2,1,0:T(8,128)S(1)}, f32[256,128]{1,0:T(8,128)S(1)}) custom-call(f32[8,3,192,128]{3,2,1,0:T(8,128)S(1)} %get-tuple-element.6.grad_ref, f32[256,128]{1,0:T(8,128)S(1)} %bitcast.9), custom_call_target="tpu_custom_call" | custom-call | tf_op jit(solution)/shard_map/pallas_call | solution.py:412
  44.2 0.7 %copy.13 = f32[2,3,64,64]{3,2,1,0:T(8,128)} copy(f32[2,3,64,64]{3,2,1,0:T(8,128)S(1)} %get-tuple-element.12) | data formatting | bytes 196608
  44.8 0.7 %copy.14 = f32[2,128,128]{2,1,0:T(8,128)} copy(f32[2,128,128]{2,1,0:T(8,128)S(1)} %bitcast.10) | data formatting | bytes 262144
Async XLA Ops:
  0.6 18.6 %copy-start = (bf16[4,2,256,256]{3,2,1,0:T(8,128)(2,1)S(1)}, bf16[4,2,256,256]{3,2,1,0:T(8,128)(2,1)}, u32[]{:S(2)}) copy-start(bf16[4,2,256,256]{3,2,1,0:T(8,128)(2,1)} %constant.2.clone.mats_ref) | copy-start | bytes 3145732
  1.4 0.9 %copy-start.1 = (f32[2,3,64,64]{3,2,1,0:T(8,128)S(1)}, f32[2,3,64,64]{3,2,1,0:T(8,128)}, u32[]{:S(2)}) copy-start(f32[2,3,64,64]{3,2,1,0:T(8,128)} %object_ref.1) | copy-start | bytes 294916
  2.3 16.9 %copy-start.2 = (f32[2,128,128]{2,1,0:T(8,128)S(1)}, f32[2,128,128]{2,1,0:T(8,128)}, u32[]{:S(2)}) copy-start(f32[2,128,128]{2,1,0:T(8,128)} %probe_ref.1) | copy-start | bytes 393220
  2.3 17.0 %copy-start.3 = (f32[1,1,2,128,128]{4,3,2,1,0:T(8,128)S(1)}, f32[1,1,2,128,128]{4,3,2,1,0:T(8,128)}, u32[]{:S(2)}) copy-start(f32[1,1,2,128,128]{4,3,2,1,0:T(8,128)} %param.10) | copy-start | bytes 393220
  2.3 17.0 %copy-start.4 = (s32[1,1,2]{2,1,0:T(1,128)S(1)}, s32[1,1,2]{2,1,0:T(1,128)}, u32[]{:S(2)}) copy-start(s32[1,1,2]{2,1,0:T(1,128)} %param.11) | copy-start | bytes 28
  2.3 17.0 %copy-start.5 = (s32[1,1,2]{2,1,0:T(1,128)S(1)}, s32[1,1,2]{2,1,0:T(1,128)}, u32[]{:S(2)}) copy-start(s32[1,1,2]{2,1,0:T(1,128)} %param.12) | copy-start | bytes 28
  2.3 17.0 %copy-start.6 = (s32[1,3]{1,0:T(1,128)S(1)}, s32[1,3]{1,0:T(1,128)}, u32[]{:S(2)}) copy-start(s32[1,3]{1,0:T(1,128)} %param.13) | copy-start | bytes 40

commit v3 on v2

--- a/solution.py
+++ b/solution.py
@@ -221,9 +221,9 @@
 
     pending = []
 
-    def upright(i, src):
-        up = to(src, spots[i], 2, z_sem.at[0, i], (me, z - 1))
-        down = to(src, spots[i], 0, z_sem.at[1, i], (me, z + 1))
+    def upright(i, j, src):
+        up = to(src, j, 2, z_sem.at[0, i], (me, z - 1))
+        down = to(src, j, 0, z_sem.at[1, i], (me, z + 1))
         pl.when(above)(lambda: up.start())
         pl.when(below)(lambda: down.start())
         pending.append((above, up))
@@ -239,33 +239,39 @@
         copy.start()
         pending.append((None, copy))
 
+    source = spots[1] + core * (spots[2] - spots[1])
+    target = spots[2] + core * (spots[1] - spots[2])
+    upright(0, me, stage)
     across(stage, me, 0, spots[1])
     across(stage, me, 1, spots[2])
-    upright(0, stage)
     share(0, 1, stage)
-    arrive(spots[1], 1)
-    upright(1, piece(spots[1], 1))
-    arrive(spots[2], 1)
-    source = spots[1] + core * (spots[2] - spots[1])
-    target = spots[2] + core * (spots[1] - spots[2])
+    arrive(source, 1)
     across(piece(source, 1), source, 2, target)
-    upright(2, piece(spots[2], 1))
+    arrive(target, 1)
+    upright(1, target, piece(target, 1))
     share(1, 1, piece(spots[1], 1))
     share(2, 1, piece(spots[2], 1))
+
+    def relay(i, j, part, when, onward=None):
+        copies = [to(piece(j, part), j, part, core_sem.at[part, i], (partner, z))]
+        if onward is not None:
+            copies.insert(0, to(piece(j, part), j, part, plane_sem.at[onward], (source, z)))
+        pending.extend((when, copy) for copy in copies)
+
+        @pl.when(when)
+        def _():
+            arrive(j, part)
+            for copy in copies:
+                copy.start()
+
+    relay(0, me, 0, above, 3)
+    relay(0, me, 2, below, 4)
     arrive(spots[3], 1)
-    upright(3, piece(spots[3], 1))
+    upright(2, spots[3], piece(spots[3], 1))
     share(3, 1, piece(spots[3], 1))
-    for i in range(4):
-        for part, when in ((0, above), (2, below)):
-
-            copy = to(piece(spots[i], part), spots[i], part, core_sem.at[part, i], (partner, z))
-            pending.append((when, copy))
-
-            @pl.when(when)
-            def _(i=i, part=part, copy=copy):
-                arrive(spots[i], part)
-                copy.start()
-
+    for i, j in ((2 - core, target), (1 + core, source), (3, spots[3])):
+        relay(i, j, 0, above)
+        relay(i, j, 2, below)
     for part, when in ((1, None), (0, above), (2, below)):
         for i in range(4):
             wait = partial(arrive, spots[i] + 1 - 2 * core, part)
@@ -276,8 +282,8 @@
 
 def reduce_kernel(
     scans, grad_ref, probe_ref, object_ref, total_ref,
-    core_in, held, z_in, ready, plane_in, last_in, passed, probe_in, scan_in, mine,
-    core_sem, z_sem, plane_sem, angle_sem, scan_sem, all_sem,
+    core_in, held, z_in, ready, plane_in, last_in, side_in, passed, probe_in, scan_in, mine,
+    core_sem, z_sem, plane_sem, side_sem, angle_sem, scan_sem, all_sem,
 ):
     angles, layers, height, lanes = grad_ref.shape
     band = height // 3
@@ -301,29 +307,44 @@
     def arrive(dst, recv_sem):
         exchange(dst, dst, core_sem.at[0, 0], recv_sem, (partner, z)).wait_recv()
 
-    order = (3, 1, 2, 0)
-    for i in order:
-        go(grad_ref.at[spots[i] + 1 - 2 * core], core_in.at[i], core_sem.at[0, i], core_sem.at[1, i], (partner, z))
+    first, second = 2 - core, 1 + core
+    near = spots[2] + core * (spots[1] - spots[2])
+    other = spots[1] + core * (spots[2] - spots[1])
+    for i, j in ((1 + core, other), (3, spots[3]), (2 - core, near), (0, me)):
+        go(grad_ref.at[j + 1 - 2 * core], core_in.at[i], core_sem.at[0, i], core_sem.at[1, i], (partner, z))
     for d, peer in enumerate(peers):
         go(
             probe_ref.at[pl.ds(peer * rows, rows)], probe_in.at[me],
             angle_sem.at[0, d], angle_sem.at[1, me], (peer, z),
         )
-    for i in order:
+    ends = (pl.ds(0, band), pl.ds(2 * band, band))
+
+    def upright(i):
+        up = exchange(
+            held.at[i, :, ends[0]], z_in.at[1, i], z_sem.at[0, 0, i], z_sem.at[1, 1, i], (me, z - 1)
+        )
+        down = exchange(
+            held.at[i, :, ends[1]], z_in.at[0, i], z_sem.at[0, 1, i], z_sem.at[1, 0, i], (me, z + 1)
+        )
+        pl.when(above)(lambda: up.start())
+        pl.when(below)(lambda: down.start())
+        pending.append((above, up))
+        pending.append((below, down))
+
+    for i, j in ((second, other), (3, spots[3]), (first, near), (0, me)):
         arrive(core_in.at[i], core_sem.at[1, i])
         for part in (0, 2, 1):
             span = pl.ds(part * band, band)
-            held[i, :, span] = grad_ref[spots[i], :, span] + core_in[i, :, span]
-        up = exchange(
-            held.at[i, :, pl.ds(0, band)], z_in.at[1, i], z_sem.at[0, 0, i], z_sem.at[1, 1, i], (me, z - 1)
-        )
-        down = exchange(
-            held.at[i, :, pl.ds(2 * band, band)], z_in.at[0, i], z_sem.at[0, 1, i], z_sem.at[1, 0, i], (me, z + 1)
-        )
-        pl.when(above)(lambda up=up: up.start())
-        pl.when(below)(lambda down=down: down.start())
-        pending.append((above, up))
-        pending.append((below, down))
+            held[i, :, span] = grad_ref[j, :, span] + core_in[i, :, span]
+        if i is second:
+            for n in range(2):
+                go(held.at[second, :, ends[n]], side_in.at[n], side_sem.at[0, n], side_sem.at[1, n], (other, z))
+        elif j is not me:
+            upright(i)
+    for n in range(2):
+        arrive(side_in.at[n], side_sem.at[1, n])
+        held[0, :, ends[n]] += side_in[n]
+    upright(0)
     for peer in peers:
         arrive(probe_in.at[peer], angle_sem.at[1, peer])
     probe_in[me] = probe_ref[pl.ds(me * rows, rows)]
@@ -334,11 +355,11 @@
     scan_in[z] = part_sum
     for d, level in enumerate(levels):
         go(passed, scan_in.at[z], scan_sem.at[0, d], scan_sem.at[1, z], (me, level))
-    first, second = 2 - core, 1 + core
-    near = spots[2] + core * (spots[1] - spots[2])
-    other = spots[1] + core * (spots[2] - spots[1])
-    for i in order:
-        ready[i] = held[i, :, pl.ds(band, band)]
+    middle = pl.ds(band, band)
+    ready[second] = held[second, :, middle]
+
+    def collect(i):
+        ready[i] = held[i, :, middle]
 
         @pl.when(above)
         def _():
@@ -350,10 +371,10 @@
             arrive(z_in.at[1, i], z_sem.at[1, 1, i])
             ready[i] += z_in[1, i]
 
-        if i == 3:
-            go(ready.at[3], plane_in.at[1], plane_sem.at[0, 1], plane_sem.at[1, 1], (near, z))
-        if i == 2:
-            go(ready.at[first], plane_in.at[0], plane_sem.at[0, 0], plane_sem.at[1, 0], (near, z))
+    collect(3)
+    go(ready.at[3], plane_in.at[1], plane_sem.at[0, 1], plane_sem.at[1, 1], (near, z))
+    collect(first)
+    go(ready.at[first], plane_in.at[0], plane_sem.at[0, 0], plane_sem.at[1, 0], (near, z))
     arrive(plane_in.at[1], plane_sem.at[1, 1])
     mine[...] = ready[second] + plane_in[1]
     go(mine, last_in, plane_sem.at[0, 2], plane_sem.at[1, 2], (other, z))
@@ -367,6 +388,7 @@
     passed_all = total_ref.at[own]
     for d, peer in enumerate(peers):
         go(passed_all, total_ref.at[own], all_sem.at[0, d], all_sem.at[1, me], (peer, z))
+    collect(0)
     arrive(plane_in.at[0], plane_sem.at[1, 0])
     arrive(last_in, plane_sem.at[1, 2])
     result = ready[0] + plane_in[0] + last_in[...]
@@ -390,7 +412,7 @@
         out_specs=vmem,
         scratch_shapes=[
             pltpu.VMEM((layers, band, 2 * width), jnp.float32),
-            dma((2, 4)), dma((3,)), dma((3, 4)), dma((3, angles)),
+            dma((2, 3)), dma((5,)), dma((3, 4)), dma((3, angles)),
         ],
         compiler_params=pltpu.CompilerParams(
             collective_id=0, has_side_effects=True, vmem_limit_bytes=32 * 2**20
@@ -419,9 +441,9 @@
         out_specs=(vmem, vmem),
         scratch_shapes=[
             buffer(4, layers, height, lanes), buffer(4, layers, height, lanes), buffer(2, 4, *block),
-            buffer(4, *block), buffer(2, *block), buffer(*block), buffer(*small),
+            buffer(4, *block), buffer(2, *block), buffer(*block), buffer(2, *block), buffer(*small),
             buffer(angles, *small), buffer(scans, *small), buffer(*block),
-            dma((2, 4)), dma((2, 2, 4)), dma((2, 3)), dma((2, angles)), dma((2, scans)),
+            dma((2, 4)), dma((2, 2, 4)), dma((2, 3)), dma((2, 2)), dma((2, angles)), dma((2, scans)),
             dma((2, angles)),
         ],
         compiler_params=pltpu.CompilerParams(

time: 45.7 us -> 44.8 us (0.980)
  Pallas kernels: 41.8 us -> 40.9 us
    pallas_call x1, Pallas kernels: 19.8 us -> 18.5 us  [reduce(): pl.pallas_call(partial(reduce_kernel, scans), out_shape=(jax.ShapeDtypeSt...]
where the time goes in v3:
time: 44.8 us; the launch traced here: 44.7 us
  Pallas kernels  40.9 us (91%)
  local copies, waits for them, and re-layouts  2.28 us (5%)
  between operations  1.47 us (3%)
    pallas_call x1, Pallas kernels, reduce(): pl.pallas_call(partial(reduce_kernel, scans), out_shape=(jax.ShapeDtypeSt...  18.5 us
    pallas_call x1, Pallas kernels, gather(): pl.pallas_call(partial(gather_kernel, scans), out_shape=jax.ShapeDtypeStr...  17.3 us
    pallas_call x1, Pallas kernels, gradients(): pl.pallas_call(partial(compute_kernel, angles), out_shape=(jax.ShapeDtype...  5.09 us
    unnamed x16, local copies, waits for them, and re-layouts  2.28 us

profile of v3, /device:TPU:0, one launch (start us, length us, event | category | flops | bytes accessed | tf_op | source)
XLA Modules:
  0.0 44.7 jit_solution(10938635623494187125)
XLA Ops:
  0.6 0.0 copy-start
  1.4 0.0 copy-start.1
  1.4 0.9 %copy-done.1 = f32[2,3,64,64]{3,2,1,0:T(8,128)S(1)} copy-done((f32[2,3,64,64]{3,2,1,0:T(8,128)S(1)}, f32[2,3,64,64]{3,2,1,0:T(8,128)}, u32[]{:S(2)}) %copy-start.1) | copy-done | bytes 98328
  2.3 0.0 copy-start.2
  2.3 0.0 copy-start.3
  2.3 0.0 copy-start.4
  2.3 0.0 copy-start.5
  2.3 0.0 copy-start.6
  2.3 17.3 %shard_map.95.region_ref = f32[8,3,192,128]{3,2,1,0:T(8,128)S(1)} custom-call(f32[2,3,64,64]{3,2,1,0:T(8,128)S(1)} %copy-done.1), custom_call_target="tpu_custom_call" | custom-call | tf_op jit(solution)/shard_map/pallas_call | solution.py:408
  19.6 0.0 copy-done
  19.7 0.0 copy-done.2
  19.7 0.0 copy-done.3
  19.7 0.0 copy-done.4
  19.7 0.0 copy-done.5
  19.7 0.0 copy-done.6
  19.7 5.1 %shard_map.96 = (f32[8,3,192,128]{3,2,1,0:T(8,128)S(1)}, f32[2,128,128]{2,1,0:T(8,128)S(1)}) custom-call(s32[2]{0:T(128)S(1)} %bitcast.11, s32[2]{0:T(128)S(1)} %bitcast.12, s32[3]{0:T(128)S(1)} %bitcast.13, s32[1]{0:T(128)} %bitcast.7.counts_ref, f32[8,3,192,128]{3,2,1,0:T(8,128)S(1)} %shard_map.95.region_ref, f32[2,128,128]{2,1,0:T(8,128)S(1)} %copy-done.2, ...), custom_call_target="tpu_custom_call" | custom-call | tf_op jit(solution)/shard_map/pallas_call | solution.py:148
  24.8 18.5 %shard_map.97 = (f32[2,3,64,64]{3,2,1,0:T(8,128)S(1)}, f32[256,128]{1,0:T(8,128)S(1)}) custom-call(f32[8,3,192,128]{3,2,1,0:T(8,128)S(1)} %get-tuple-element.6.grad_ref, f32[256,128]{1,0:T(8,128)S(1)} %bitcast.9), custom_call_target="tpu_custom_call" | custom-call | tf_op jit(solution)/shard_map/pallas_call | solution.py:434
  43.4 0.7 %copy.13 = f32[2,3,64,64]{3,2,1,0:T(8,128)} copy(f32[2,3,64,64]{3,2,1,0:T(8,128)S(1)} %get-tuple-element.12) | data formatting | bytes 196608
  44.0 0.7 %copy.14 = f32[2,128,128]{2,1,0:T(8,128)} copy(f32[2,128,128]{2,1,0:T(8,128)S(1)} %bitcast.10) | data formatting | bytes 262144
Async XLA Ops:
  0.6 19.0 %copy-start = (bf16[4,2,256,256]{3,2,1,0:T(8,128)(2,1)S(1)}, bf16[4,2,256,256]{3,2,1,0:T(8,128)(2,1)}, u32[]{:S(2)}) copy-start(bf16[4,2,256,256]{3,2,1,0:T(8,128)(2,1)} %constant.2.clone.mats_ref) | copy-start | bytes 3145732
  1.4 0.9 %copy-start.1 = (f32[2,3,64,64]{3,2,1,0:T(8,128)S(1)}, f32[2,3,64,64]{3,2,1,0:T(8,128)}, u32[]{:S(2)}) copy-start(f32[2,3,64,64]{3,2,1,0:T(8,128)} %object_ref.1) | copy-start | bytes 294916
  2.3 17.3 %copy-start.2 = (f32[2,128,128]{2,1,0:T(8,128)S(1)}, f32[2,128,128]{2,1,0:T(8,128)}, u32[]{:S(2)}) copy-start(f32[2,128,128]{2,1,0:T(8,128)} %probe_ref.1) | copy-start | bytes 393220
  2.3 17.4 %copy-start.3 = (f32[1,1,2,128,128]{4,3,2,1,0:T(8,128)S(1)}, f32[1,1,2,128,128]{4,3,2,1,0:T(8,128)}, u32[]{:S(2)}) copy-start(f32[1,1,2,128,128]{4,3,2,1,0:T(8,128)} %param.10) | copy-start | bytes 393220
  2.3 17.4 %copy-start.4 = (s32[1,1,2]{2,1,0:T(1,128)S(1)}, s32[1,1,2]{2,1,0:T(1,128)}, u32[]{:S(2)}) copy-start(s32[1,1,2]{2,1,0:T(1,128)} %param.11) | copy-start | bytes 28
  2.3 17.4 %copy-start.5 = (s32[1,1,2]{2,1,0:T(1,128)S(1)}, s32[1,1,2]{2,1,0:T(1,128)}, u32[]{:S(2)}) copy-start(s32[1,1,2]{2,1,0:T(1,128)} %param.12) | copy-start | bytes 28
  2.3 17.4 %copy-start.6 = (s32[1,3]{1,0:T(1,128)S(1)}, s32[1,3]{1,0:T(1,128)}, u32[]{:S(2)}) copy-start(s32[1,3]{1,0:T(1,128)} %param.13) | copy-start | bytes 40
